TPU v7x, 32 devices: a whole 2x2x4 slice. The times are simulated.
32 devices in a mesh: dp: 32 (over z, y, x, core), tensor: 1.
Axes of the slice: x: 2, y: 2, z: 4, core: 2. Of those that a mesh axis runs over, the one named last changes fastest.
Arguments:
- activations: bfloat16 [384, 8192], P('dp', 'tensor'), may hold values from -400 to 400, as said below
- weight: bfloat16 [8192, 28672], P('dp', 'tensor'), may hold values from -0.0625 to 0.0625
Outputs:
- channel_mean: float32 [8192], P('dp')
- column_errors: float32 [4, 28672], P(None, ('tensor', 'dp'))
- errors: float32 [4], replicated
Inputs may be any that keep to these rules, and one draw needn't show every extreme that they name: activations and weight are finite real values within the ranges stated above.
All inputs are finite; a program needn't handle non-finite values.
Results may differ from a plain program's by a relative error of at most 0.0012.
The roundings to bfloat16 on the way count: a program that leaves them out, or rounds other values in their place, can miss the bound.
Values may be sent and summed in bfloat16 or wider, within the bound.
A program may use at most 128 MiB of HBM per device.

v0:
```python
import math
import jax
import jax.numpy as jnp
from jax import lax
from jax.sharding import PartitionSpec as P

D = 8192
F = 28672
GROUP = 128
GRID = 4


def soft_round(values):
    return values - jnp.sin(2.0 * math.pi * values) / (2.0 * math.pi)


def scale_table(channel_mean):
    ratios = jnp.arange(GRID, dtype=jnp.float32) / GRID
    raw = jnp.exp(ratios[:, None] * jnp.log(channel_mean)[None, :])
    top = jnp.max(raw, axis=1, keepdims=True)
    bottom = jnp.min(raw, axis=1, keepdims=True)
    return raw / jnp.sqrt(top * bottom)


def on_device(activations, weight):
    widened = lax.all_gather(activations, "tensor", axis=1, tiled=True)
    gathered = lax.all_gather(widened, "dp", axis=0, tiled=True)
    columns = lax.all_to_all(weight, "dp", split_axis=1, concat_axis=0, tiled=True)
    width = columns.shape[1]
    token_count = gathered.shape[0]
    channel_mean = jnp.sum(jnp.abs(gathered), axis=0, dtype=jnp.float32) / token_count + 1e-06
    scales = scale_table(channel_mean)
    base_out = jnp.dot(gathered, columns, preferred_element_type=jnp.float32)
    weight_float = columns.astype(jnp.float32)

    def local_error(factor):
        scaled = weight_float * factor[:, None]
        grouped = scaled.reshape(D // GROUP, GROUP, width)
        quant_step = (jnp.max(jnp.abs(grouped), axis=1, keepdims=True) + 1e-06) / 7.0
        levels = soft_round(grouped / quant_step)
        dequant = ((levels * quant_step).reshape(D, width) / factor[:, None]).astype(jnp.bfloat16)
        quant_out = jnp.dot(gathered, dequant, preferred_element_type=jnp.float32)
        residue = quant_out - base_out
        return jnp.sum(residue * residue, axis=0)

    column_sums = lax.map(local_error, scales)
    totals = lax.psum(jnp.sum(column_sums, axis=1), ("dp", "tensor"))
    errors = totals / (token_count * F)
    column_errors = column_sums / token_count
    rows = D // lax.axis_size("dp")
    own_mean = lax.dynamic_slice_in_dim(channel_mean, lax.axis_index("dp") * rows, rows)
    return (own_mean, column_errors, errors)


def solution(mesh):
    placed = (P("dp", "tensor"), P("dp", "tensor"))
    return jax.shard_map(
        on_device,
        mesh=mesh,
        in_specs=placed,
        out_specs=(P("dp"), P(None, ("tensor", "dp")), P()),
        check_vma=False,
    )
```

profile of v0, /device:TPU:10, one launch (start us, length us, event | category | flops | bytes accessed | tf_op | source)
XLA Modules:
  0.0 1007.1 jit_solution(17672235524525206103)
XLA Ops:
  7.2 14.7 %copy.10 = bf16[32,32,8,896]{3,2,0,1:T(8,128)(2,1)} copy(bf16[32,32,8,896]{3,2,1,0:T(8,128)(2,1)} %bitcast.49) | data formatting | bytes 29360128 | tf_op jit(solution)/shard_map/all_to_all | solution.py:28
  21.9 6.1 all-to-all-start
  28.7 192.3 %all-gather.3.cloned.1.call-done = bf16[32,12,8192]{2,1,0:T(8,128)(2,1)} async-done(((bf16[1,12,8192]{2,1,0:T(8,128)(2,1)}), bf16[32,12,8192]{2,1,0:T(8,128)(2,1)}) %all-gather.3.cloned.1.call-update) | async-done | bytes 6291472 | tf_op jit(solution)/shard_map/all_gather | solution.py:27
  221.0 8.8 reshape.50
  235.0 147.9 %all-to-all-done = bf16[256,32,896]{2,0,1:T(8,128)(2,1)} async-done(((bf16[256,32,896]{2,0,1:T(8,128)(2,1)}), bf16[256,32,896]{2,0,1:T(8,128)(2,1)}, u32[]{:S(2)}, u32[]{:S(2)}) %all-to-all-start) | async-done | bytes 14680096 | tf_op jit(solution)/shard_map/all_to_all | solution.py:28
  382.9 12.0 %fusion.10 = f32[384,896]{1,0:T(8,128)} fusion(bf16[384,8192]{1,0:T(8,128)(2,1)} %reshape.50, bf16[8192,896]{1,0:T(8,128)(2,1)} %bitcast.7), kind=kOutput, calls=%fused_computation.25 | convolution fusion | flops 5637144576 | bytes 22347776 | tf_op jit(solution)/shard_map/dot_general | solution.py:33
  394.9 16.6 %bitcast_convert_fusion = f32[8192,896]{1,0:T(8,128)} fusion(bf16[256,32,896]{2,0,1:T(8,128)(2,1)} %all-to-all-done), kind=kLoop, calls=%fused_computation.22 | loop fusion | flops 7340032 | bytes 44040192 | tf_op jit(solution)/shard_map/convert_element_type | solution.py:34
  411.4 541.8 %while.10 = (s32[]{:T(128)}, f32[4,896]{1,0:T(4,128)S(1)}, f32[4,8192]{1,0:T(4,128)S(1)}, f32[8192,896]{1,0:T(8,128)}, bf16[384,8192]{1,0:T(8,128)(2,1)}, /*index=5*/f32[384,896]{1,0:T(8,128)}, s32[]{:T(128)}, s32[]{:T(128)}) while((s32[]{:T(128)}, f32[4,896]{1,0:T(4,128)S(1)}, f32[4,8192]{1,0:T(4,128)S(1)}, f32[8192,896]{1,0:T(8,128)}, ...), condition=%wide.region_6.7_spmd, body=%wide.region_3.6_spmd.sunk | while | flops 5718973440 | bytes 214255232 | solution.py:46
  411.5 12.5 %abs_reduce_fusion.2 = f32[64,896]{1,0:T(8,128)S(1)} fusion(f32[64,128]{1,0:T(8,128)S(1)} %bitcast.50, f32[8192,896]{1,0:T(8,128)} %get-tuple-element.110), kind=kLoop, calls=%fused_computation.4.clone.1 | loop fusion | flops 21962752 | bytes 29622272 | tf_op jit(solution)/shard_map/while/body/eval_jaxpr/reduce_max | solution.py:39
  424.0 5.2 copy-done
  429.2 108.3 %fusion.21 = bf16[8192,896]{1,0:T(8,128)(2,1)S(1)} fusion(f32[8192,896]{1,0:T(8,128)S(1)} %copy-done, f32[64,896]{1,0:T(8,128)S(1)} %add_multiply_fusion.2, f32[8192]{0:T(1024)S(1)} %bitcast.51), kind=kLoop, calls=%fused_computation.3.clone.1 | loop fusion | flops 58720256 | bytes 44302336 | tf_op jit(solution)/shard_map/while/body/eval_jaxpr/convert_element_type | solution.py:41
  537.5 9.3 fusion.22
  546.9 12.5 %abs_reduce_fusion.2 = f32[64,896]{1,0:T(8,128)S(1)} fusion(f32[64,128]{1,0:T(8,128)S(1)} %bitcast.50, f32[8192,896]{1,0:T(8,128)} %get-tuple-element.110), kind=kLoop, calls=%fused_computation.4.clone.1 | loop fusion | flops 21962752 | bytes 29622272 | tf_op jit(solution)/shard_map/while/body/eval_jaxpr/reduce_max | solution.py:39
  559.4 5.2 copy-done
  564.7 108.3 %fusion.21 = bf16[8192,896]{1,0:T(8,128)(2,1)S(1)} fusion(f32[8192,896]{1,0:T(8,128)S(1)} %copy-done, f32[64,896]{1,0:T(8,128)S(1)} %add_multiply_fusion.2, f32[8192]{0:T(1024)S(1)} %bitcast.51), kind=kLoop, calls=%fused_computation.3.clone.1 | loop fusion | flops 58720256 | bytes 44302336 | tf_op jit(solution)/shard_map/while/body/eval_jaxpr/convert_element_type | solution.py:41
  673.0 9.2 fusion.22
  682.4 12.5 %abs_reduce_fusion.2 = f32[64,896]{1,0:T(8,128)S(1)} fusion(f32[64,128]{1,0:T(8,128)S(1)} %bitcast.50, f32[8192,896]{1,0:T(8,128)} %get-tuple-element.110), kind=kLoop, calls=%fused_computation.4.clone.1 | loop fusion | flops 21962752 | bytes 29622272 | tf_op jit(solution)/shard_map/while/body/eval_jaxpr/reduce_max | solution.py:39
  700.1 108.3 %fusion.21 = bf16[8192,896]{1,0:T(8,128)(2,1)S(1)} fusion(f32[8192,896]{1,0:T(8,128)S(1)} %copy-done, f32[64,896]{1,0:T(8,128)S(1)} %add_multiply_fusion.2, f32[8192]{0:T(1024)S(1)} %bitcast.51), kind=kLoop, calls=%fused_computation.3.clone.1 | loop fusion | flops 58720256 | bytes 44302336 | tf_op jit(solution)/shard_map/while/body/eval_jaxpr/convert_element_type | solution.py:41
  808.4 9.3 fusion.22
  817.8 12.5 %abs_reduce_fusion.2 = f32[64,896]{1,0:T(8,128)S(1)} fusion(f32[64,128]{1,0:T(8,128)S(1)} %bitcast.50, f32[8192,896]{1,0:T(8,128)} %get-tuple-element.110), kind=kLoop, calls=%fused_computation.4.clone.1 | loop fusion | flops 21962752 | bytes 29622272 | tf_op jit(solution)/shard_map/while/body/eval_jaxpr/reduce_max | solution.py:39
  830.3 5.2 copy-done
  835.6 108.3 %fusion.21 = bf16[8192,896]{1,0:T(8,128)(2,1)S(1)} fusion(f32[8192,896]{1,0:T(8,128)S(1)} %copy-done, f32[64,896]{1,0:T(8,128)S(1)} %add_multiply_fusion.2, f32[8192]{0:T(1024)S(1)} %bitcast.51), kind=kLoop, calls=%fused_computation.3.clone.1 | loop fusion | flops 58720256 | bytes 44302336 | tf_op jit(solution)/shard_map/while/body/eval_jaxpr/convert_element_type | solution.py:41
  943.9 9.3 fusion.22
  954.0 45.8 %psum.7 = f32[4]{0:T(128)S(1)} all-reduce(f32[4]{0:T(128)S(1)} %get-tuple-element.52), channel_id=1, replica_groups=mesh['dp'=32,'tensor'=1] {'dp','tensor'}, use_global_device_ids=true, to_apply=%region_8.9 | all-reduce | flops 4 | bytes 32 | tf_op jit(solution)/shard_map/psum | solution.py:47
  (33 shorter events, 13.0 us)
Async XLA Ops:
  21.9 361.0 %all-to-all-start = ((bf16[256,32,896]{2,0,1:T(8,128)(2,1)}), bf16[256,32,896]{2,0,1:T(8,128)(2,1)}, u32[]{:S(2)}, u32[]{:S(2)}) async-start(bf16[256,32,896]{2,0,1:T(8,128)(2,1)} %bitcast.48), calls=%async_computation | async-start | bytes 29360128 | tf_op jit(solution)/shard_map/all_to_all | solution.py:28
  27.9 193.0 %all-gather.3.cloned.1.call-start = ((), (), s32[]{:S(2)}) async-start(), calls=%async_computation.1 | async-start | bytes 8650752 | tf_op jit(solution)/shard_map/all_gather | solution.py:27
  411.5 17.8 %copy-start = (f32[8192,896]{1,0:T(8,128)S(1)}, f32[8192,896]{1,0:T(8,128)}, u32[]{:S(2)}) copy-start(f32[8192,896]{1,0:T(8,128)} %get-tuple-element.110) | copy-start | bytes 88080384 | tf_op jit(solution)/shard_map/while
  546.9 17.8 %copy-start = (f32[8192,896]{1,0:T(8,128)S(1)}, f32[8192,896]{1,0:T(8,128)}, u32[]{:S(2)}) copy-start(f32[8192,896]{1,0:T(8,128)} %get-tuple-element.110) | copy-start | bytes 88080384 | tf_op jit(solution)/shard_map/while
  682.4 17.8 %copy-start = (f32[8192,896]{1,0:T(8,128)S(1)}, f32[8192,896]{1,0:T(8,128)}, u32[]{:S(2)}) copy-start(f32[8192,896]{1,0:T(8,128)} %get-tuple-element.110) | copy-start | bytes 88080384 | tf_op jit(solution)/shard_map/while
  817.8 17.8 %copy-start = (f32[8192,896]{1,0:T(8,128)S(1)}, f32[8192,896]{1,0:T(8,128)}, u32[]{:S(2)}) copy-start(f32[8192,896]{1,0:T(8,128)} %get-tuple-element.110) | copy-start | bytes 88080384 | tf_op jit(solution)/shard_map/while
Sparse Core Ops, SparseCore 0:
  31.6 189.3 all-gather.2
where the time goes:
time: 1010 us
  other arithmetic  506 us (50%)
  waiting for transfers between devices  341 us (34%)
  matrix products  49 us (5%)
  blocking collectives  45.8 us (5%)
  local copies, waits for them, and re-layouts  45.5 us (5%)
  between operations  14.1 us (1%)
    convert_element_type x4, other arithmetic, local_error(): ((levels * quant_step).reshape(D, width) / factor[:, None]).astype(jnp.bf...  433 us
    all_gather x1, waiting for transfers between devices, on_device(): gathered = lax.all_gather(widened, 'dp', axis=0, tiled=True)  192 us
    all_to_all x1, waiting for transfers between devices, on_device(): lax.all_to_all(weight, 'dp', split_axis=1, concat_axis=0, tiled=True)  148 us
    reduce_max x4, other arithmetic, local_error(): jnp.max(jnp.abs(grouped), axis=1, keepdims=True) + 1e-06  49.8 us
    psum x1, blocking collectives, on_device(): totals = lax.psum(jnp.sum(column_sums, axis=1), ('dp', 'tensor'))  45.8 us
    dot_general x4, matrix products, local_error(): quant_out = jnp.dot(gathered, dequant, preferred_element_type=jnp.float32)  37 us
    while x8, local copies, waits for them, and re-layouts  21 us
  transfers between devices with their start and end apart: 2, of which 2 were waited for; matrix products, arithmetic and copies ran while one was open for 1% of the time, Pallas kernels for 0%

commit v1 on v0

--- a/solution.py
+++ b/solution.py
@@ -25,7 +25,10 @@
 def on_device(activations, weight):
     widened = lax.all_gather(activations, "tensor", axis=1, tiled=True)
     gathered = lax.all_gather(widened, "dp", axis=0, tiled=True)
-    columns = lax.all_to_all(weight, "dp", split_axis=1, concat_axis=0, tiled=True)
+    columns = jnp.concatenate(
+        lax.all_to_all(jnp.stack(jnp.split(weight, lax.axis_size("dp"), axis=1)), "dp", 0, 0),
+        axis=0,
+    )
     width = columns.shape[1]
     token_count = gathered.shape[0]
     channel_mean = jnp.sum(jnp.abs(gathered), axis=0, dtype=jnp.float32) / token_count + 1e-06

time: 1010 us -> 1050 us (1.040)
  local copies, waits for them, and re-layouts: 45.5 us -> 91 us
    unnamed x1 -> x32, local copies, waits for them, and re-layouts: 8.77 us -> 65.6 us
    all_to_all x1 -> x0, local copies, waits for them, and re-layouts: 14.7 us -> none  [on_device(): lax.all_to_all(weight, 'dp', split_axis=1, concat_axis=0, tiled=True)]
    while x8 -> x9, local copies, waits for them, and re-layouts: 21 us -> 22.5 us
where the time goes in v1:
time: 1050 us
  other arithmetic  506 us (48%)
  waiting for transfers between devices  341 us (32%)
  local copies, waits for them, and re-layouts  91 us (9%)
  matrix products  49 us (5%)
  blocking collectives  45.8 us (4%)
  between operations  14.1 us (1%)
    convert_element_type x4, other arithmetic, local_error(): ((levels * quant_step).reshape(D, width) / factor[:, None]).astype(jnp.bf...  433 us
    all_gather x1, waiting for transfers between devices, on_device(): gathered = lax.all_gather(widened, 'dp', axis=0, tiled=True)  192 us
    all_to_all x1, waiting for transfers between devices, on_device(): lax.all_to_all(jnp.stack(jnp.split(weight, lax.axis_size('dp'), axis=1)),...  148 us
    unnamed x32, local copies, waits for them, and re-layouts  65.6 us
    reduce_max x4, other arithmetic, local_error(): jnp.max(jnp.abs(grouped), axis=1, keepdims=True) + 1e-06  49.8 us
    psum x1, blocking collectives, on_device(): totals = lax.psum(jnp.sum(column_sums, axis=1), ('dp', 'tensor'))  45.8 us
    dot_general x4, matrix products, local_error(): quant_out = jnp.dot(gathered, dequant, preferred_element_type=jnp.float32)  37 us
  transfers between devices with their start and end apart: 2, of which 2 were waited for; matrix products, arithmetic and copies ran while one was open for 1% of the time, Pallas kernels for 0%

profile of v1, /device:TPU:10, one launch (start us, length us, event | category | flops | bytes accessed | tf_op | source)
XLA Modules:
  0.0 1052.7 jit_solution(4435498827576402804)
XLA Ops:
  65.9 6.1 all-to-all-start
  72.7 192.3 %all-gather.3.cloned.1.call-done = bf16[32,12,8192]{2,1,0:T(8,128)(2,1)} async-done(((bf16[1,12,8192]{2,1,0:T(8,128)(2,1)}), bf16[32,12,8192]{2,1,0:T(8,128)(2,1)}) %all-gather.3.cloned.1.call-update) | async-done | bytes 6291472 | tf_op jit(solution)/shard_map/all_gather | solution.py:27
  265.0 8.8 reshape.51
  279.0 147.9 %all-to-all-done = bf16[32,256,896]{2,1,0:T(8,128)(2,1)} async-done(((bf16[32,256,896]{2,1,0:T(8,128)(2,1)}), bf16[32,256,896]{2,1,0:T(8,128)(2,1)}, u32[]{:S(2)}, u32[]{:S(2)}) %all-to-all-start) | async-done | bytes 14680096 | tf_op jit(solution)/shard_map/all_to_all | solution.py:29
  426.9 12.0 %convolution_bitcast_fusion.1 = f32[384,896]{0,1:T(8,128)S(1)} fusion(bf16[8192,896]{1,0:T(8,128)(2,1)} %bitcast.38, bf16[384,8192]{1,0:T(8,128)(2,1)} %reshape.51), kind=kOutput, calls=%fused_computation.12 | convolution fusion | flops 5637144576 | bytes 22347776 | tf_op jit(solution)/shard_map/dot_general | solution.py:36
  440.5 16.6 %bitcast_convert_fusion = f32[8192,896]{1,0:T(8,128)} fusion(bf16[32,256,896]{2,1,0:T(8,128)(2,1)} %all-to-all-done), kind=kLoop, calls=%fused_computation.54 | loop fusion | flops 7340032 | bytes 44040192 | tf_op jit(solution)/shard_map/convert_element_type | solution.py:37
  457.0 541.8 %while.10 = (s32[]{:T(128)}, f32[4,896]{1,0:T(4,128)S(1)}, f32[4,8192]{1,0:T(4,128)S(1)}, f32[8192,896]{1,0:T(8,128)}, bf16[384,8192]{1,0:T(8,128)(2,1)}, /*index=5*/f32[384,896]{1,0:T(8,128)}, s32[]{:T(128)}, s32[]{:T(128)}) while((s32[]{:T(128)}, f32[4,896]{1,0:T(4,128)S(1)}, f32[4,8192]{1,0:T(4,128)S(1)}, f32[8192,896]{1,0:T(8,128)}, ...), condition=%wide.region_6.7_spmd, body=%wide.region_3.6_spmd.sunk | while | flops 5718973440 | bytes 214255232 | solution.py:49
  457.1 12.5 %abs_reduce_fusion.2 = f32[64,896]{1,0:T(8,128)S(1)} fusion(f32[64,128]{1,0:T(8,128)S(1)} %bitcast.108, f32[8192,896]{1,0:T(8,128)} %get-tuple-element.128), kind=kLoop, calls=%fused_computation.4.clone.1 | loop fusion | flops 21962752 | bytes 29622272 | tf_op jit(solution)/shard_map/while/body/eval_jaxpr/reduce_max | solution.py:42
  469.6 5.2 copy-done
  474.8 108.3 %fusion.20 = bf16[8192,896]{1,0:T(8,128)(2,1)S(1)} fusion(f32[8192,896]{1,0:T(8,128)S(1)} %copy-done, f32[64,896]{1,0:T(8,128)S(1)} %add_multiply_fusion.2, f32[8192]{0:T(1024)S(1)} %bitcast.109), kind=kLoop, calls=%fused_computation.3.clone.1 | loop fusion | flops 58720256 | bytes 44302336 | tf_op jit(solution)/shard_map/while/body/eval_jaxpr/convert_element_type | solution.py:44
  583.1 9.2 fusion.21
  592.5 12.5 %abs_reduce_fusion.2 = f32[64,896]{1,0:T(8,128)S(1)} fusion(f32[64,128]{1,0:T(8,128)S(1)} %bitcast.108, f32[8192,896]{1,0:T(8,128)} %get-tuple-element.128), kind=kLoop, calls=%fused_computation.4.clone.1 | loop fusion | flops 21962752 | bytes 29622272 | tf_op jit(solution)/shard_map/while/body/eval_jaxpr/reduce_max | solution.py:42
  605.0 5.2 copy-done
  610.3 108.3 %fusion.20 = bf16[8192,896]{1,0:T(8,128)(2,1)S(1)} fusion(f32[8192,896]{1,0:T(8,128)S(1)} %copy-done, f32[64,896]{1,0:T(8,128)S(1)} %add_multiply_fusion.2, f32[8192]{0:T(1024)S(1)} %bitcast.109), kind=kLoop, calls=%fused_computation.3.clone.1 | loop fusion | flops 58720256 | bytes 44302336 | tf_op jit(solution)/shard_map/while/body/eval_jaxpr/convert_element_type | solution.py:44
  718.6 9.3 fusion.21
  728.0 12.5 %abs_reduce_fusion.2 = f32[64,896]{1,0:T(8,128)S(1)} fusion(f32[64,128]{1,0:T(8,128)S(1)} %bitcast.108, f32[8192,896]{1,0:T(8,128)} %get-tuple-element.128), kind=kLoop, calls=%fused_computation.4.clone.1 | loop fusion | flops 21962752 | bytes 29622272 | tf_op jit(solution)/shard_map/while/body/eval_jaxpr/reduce_max | solution.py:42
  740.5 5.2 copy-done
  745.7 108.3 %fusion.20 = bf16[8192,896]{1,0:T(8,128)(2,1)S(1)} fusion(f32[8192,896]{1,0:T(8,128)S(1)} %copy-done, f32[64,896]{1,0:T(8,128)S(1)} %add_multiply_fusion.2, f32[8192]{0:T(1024)S(1)} %bitcast.109), kind=kLoop, calls=%fused_computation.3.clone.1 | loop fusion | flops 58720256 | bytes 44302336 | tf_op jit(solution)/shard_map/while/body/eval_jaxpr/convert_element_type | solution.py:44
  854.0 9.3 fusion.21
  863.4 12.5 %abs_reduce_fusion.2 = f32[64,896]{1,0:T(8,128)S(1)} fusion(f32[64,128]{1,0:T(8,128)S(1)} %bitcast.108, f32[8192,896]{1,0:T(8,128)} %get-tuple-element.128), kind=kLoop, calls=%fused_computation.4.clone.1 | loop fusion | flops 21962752 | bytes 29622272 | tf_op jit(solution)/shard_map/while/body/eval_jaxpr/reduce_max | solution.py:42
  875.9 5.2 copy-done
  881.2 108.3 %fusion.20 = bf16[8192,896]{1,0:T(8,128)(2,1)S(1)} fusion(f32[8192,896]{1,0:T(8,128)S(1)} %copy-done, f32[64,896]{1,0:T(8,128)S(1)} %add_multiply_fusion.2, f32[8192]{0:T(1024)S(1)} %bitcast.109), kind=kLoop, calls=%fused_computation.3.clone.1 | loop fusion | flops 58720256 | bytes 44302336 | tf_op jit(solution)/shard_map/while/body/eval_jaxpr/convert_element_type | solution.py:44
  989.5 9.3 fusion.21
  999.5 45.8 %psum.7 = f32[4]{0:T(128)S(1)} all-reduce(f32[4]{0:T(128)S(1)} %get-tuple-element.70), channel_id=1, replica_groups=mesh['dp'=32,'tensor'=1] {'dp','tensor'}, use_global_device_ids=true, to_apply=%region_8.9 | all-reduce | flops 4 | bytes 32 | tf_op jit(solution)/shard_map/psum | solution.py:50
  (65 shorter events, 67.9 us)
Async XLA Ops:
  65.9 361.0 %all-to-all-start = ((bf16[32,256,896]{2,1,0:T(8,128)(2,1)}), bf16[32,256,896]{2,1,0:T(8,128)(2,1)}, u32[]{:S(2)}, u32[]{:S(2)}) async-start(bf16[32,256,896]{2,1,0:T(8,128)(2,1)} %bitcast_dynamic-update-slice_fusion), calls=%async_computation | async-start | bytes 29360128 | tf_op jit(solution)/shard_map/all_to_all | solution.py:29
  71.9 193.0 %all-gather.3.cloned.1.call-start = ((), (), s32[]{:S(2)}) async-start(), calls=%async_computation.1 | async-start | bytes 8650752 | tf_op jit(solution)/shard_map/all_gather | solution.py:27
  457.1 17.8 %copy-start = (f32[8192,896]{1,0:T(8,128)S(1)}, f32[8192,896]{1,0:T(8,128)}, u32[]{:S(2)}) copy-start(f32[8192,896]{1,0:T(8,128)} %get-tuple-element.128) | copy-start | bytes 88080384 | tf_op jit(solution)/shard_map/while
  592.5 17.8 %copy-start = (f32[8192,896]{1,0:T(8,128)S(1)}, f32[8192,896]{1,0:T(8,128)}, u32[]{:S(2)}) copy-start(f32[8192,896]{1,0:T(8,128)} %get-tuple-element.128) | copy-start | bytes 88080384 | tf_op jit(solution)/shard_map/while
  728.0 17.8 %copy-start = (f32[8192,896]{1,0:T(8,128)S(1)}, f32[8192,896]{1,0:T(8,128)}, u32[]{:S(2)}) copy-start(f32[8192,896]{1,0:T(8,128)} %get-tuple-element.128) | copy-start | bytes 88080384 | tf_op jit(solution)/shard_map/while
  863.4 17.8 %copy-start = (f32[8192,896]{1,0:T(8,128)S(1)}, f32[8192,896]{1,0:T(8,128)}, u32[]{:S(2)}) copy-start(f32[8192,896]{1,0:T(8,128)} %get-tuple-element.128) | copy-start | bytes 88080384 | tf_op jit(solution)/shard_map/while
Sparse Core Ops, SparseCore 0:
  75.6 189.3 all-gather.2
